TPU v7x, 32 devices: a whole 2x2x4 slice. The times are simulated.
32 devices in a mesh: dom: 4 (over z), col: 8 (over y, x, core).
Axes of the slice: x: 2, y: 2, z: 4, core: 2. Of those that a mesh axis runs over, the one named last changes fastest.
Arguments:
- rhs_interior: bfloat16 [4, 48, 8192], P('dom', 'col'), may hold values from -6 to 6
- interior_inv: bfloat16 [4, 8192, 8192], P('dom', None, 'col'), may hold values from -0.0625 to 0.0625
- coupling: bfloat16 [4, 8192, 768], P('dom', 'col'), may hold values from -0.0625 to 0.0625
- rhs_interface: bfloat16 [48, 8192], P('col', 'dom'), may hold values from -6 to 6
- block_ids: int32 [4, 6], P('dom'), may hold values from 0 to 63, as said below
- interface_inv: bfloat16 [8192, 8192], P('dom', 'col'), may hold values from -0.0625 to 0.0625
Outputs:
- interior_solution: bfloat16 [4, 48, 8192], P('dom', None, 'col')
- interface_solution: bfloat16 [48, 8192], P('col')
Inputs may be any that keep to these rules, and one draw needn't show every extreme that they name: `block_ids`: each row names 6 different blocks.
All inputs are finite; a program needn't handle non-finite values.
Results may differ from a plain program's by a relative error of at most 0.025.
Values may be sent and summed in bfloat16 or wider, within the bound.
No kernel may reach another device: no remote copies, remote signals or barrier semaphores. Data moves between devices by JAX's collectives and lax.ppermute only.
A program may use at most 64 MiB of HBM per device.

v0:
```python
import jax
import jax.numpy as jnp
from jax import lax
from jax.sharding import PartitionSpec as P

G = 8192
BS = 128


def per_device(rhs_interior, interior_inv, coupling, rhs_interface, block_ids, interface_inv):
    rhs_local = rhs_interior[0]
    inverse = interior_inv[0]
    couple = coupling[0]
    blocks = block_ids[0]
    row_count = rhs_local.shape[0]
    block_count = blocks.shape[0]
    nblocks = G // BS
    onehot = (blocks[:, None] == jnp.arange(nblocks, dtype=jnp.int32)[None, :]).astype(jnp.float32)
    interior_step = jnp.dot(
        lax.all_gather(rhs_local, "col", axis=0, tiled=True),
        inverse,
        preferred_element_type=jnp.float32,
    ).astype(jnp.bfloat16)
    contribution = lax.psum_scatter(
        jnp.dot(interior_step, couple, preferred_element_type=jnp.float32).astype(jnp.bfloat16),
        "col",
        scatter_dimension=0,
        tiled=True,
    ).astype(jnp.float32)
    placed = jnp.einsum(
        "kb,rks->rbs", onehot, contribution.reshape(row_count, block_count, BS)
    ).reshape(row_count, G)
    summed = lax.psum_scatter(
        placed.astype(jnp.bfloat16), "dom", scatter_dimension=1, tiled=True
    ).astype(jnp.float32)
    reduced = (rhs_interface.astype(jnp.float32) - summed).astype(jnp.bfloat16)
    partial_solution = jnp.dot(
        lax.all_gather(reduced, "col", axis=0, tiled=True),
        interface_inv,
        preferred_element_type=jnp.float32,
    )
    column_total = lax.psum(partial_solution.astype(jnp.bfloat16), "dom")
    solution = lax.all_to_all(column_total, "col", split_axis=0, concat_axis=1, tiled=True)
    local_solution = jnp.einsum(
        "kb,rbs->rks",
        onehot.astype(jnp.bfloat16),
        solution.reshape(row_count, nblocks, BS),
        preferred_element_type=jnp.float32,
    )
    local_solution = local_solution.reshape(row_count, block_count * BS).astype(jnp.bfloat16)
    every_solution = lax.all_gather(local_solution, "col", axis=0, tiled=True)
    correction = jnp.einsum("rl,il->ri", every_solution, couple, preferred_element_type=jnp.float32)
    rhs_columns = lax.all_to_all(rhs_local, "col", split_axis=1, concat_axis=0, tiled=True)
    interior_rhs = (rhs_columns.astype(jnp.float32) - correction).astype(jnp.bfloat16)
    result = jnp.dot(
        lax.all_gather(interior_rhs, "col", axis=1, tiled=True),
        inverse,
        preferred_element_type=jnp.float32,
    )
    interior_solution = result.astype(jnp.bfloat16)[None]
    return (interior_solution, solution)


def solution(mesh):
    placed = (
        P("dom", "col", None),
        P("dom", None, "col"),
        P("dom", "col", None),
        P("col", "dom"),
        P("dom", None),
        P("dom", "col"),
    )
    return jax.shard_map(
        per_device,
        mesh=mesh,
        in_specs=placed,
        out_specs=(P("dom", None, "col"), P("col", None)),
        check_vma=False,
    )
```

profile of v0, /device:TPU:0, one launch (start us, length us, event | category | flops | bytes accessed | tf_op | source)
XLA Modules:
  0.0 168.0 jit_solution(9237124908893844768)
XLA Ops:
  7.2 0.0 copy-start
  7.2 0.0 reduce-scatter.4.cloned.1.call-start
  7.2 1.2 copy.15
  8.4 14.6 %all-gather = bf16[1,48,8192]{2,0,1:T(2,128)(2,1)S(1)} all-gather(bf16[1,6,8192]{2,0,1:T(2,128)(2,1)S(1)} %copy.15), channel_id=2, replica_groups=mesh['dom'=4,'col'=8] {'col'}, dimensions={1}, use_global_device_ids=true | all-gather | bytes 884736 | tf_op jit(solution)/shard_map/all_gather | solution.py:20
  23.0 0.0 copy-done
  23.0 0.0 copy-start.3
  23.0 0.0 copy-start.4
  23.0 0.0 copy-start.2
  23.0 9.5 %fusion.21 = bf16[48,768]{1,0:T(8,128)(2,1)S(1)} fusion(bf16[1,1024,768]{2,1,0:T(8,128)(2,1)S(1)} %copy-done, bf16[1,8192,1024]{2,1,0:T(8,128)(2,1)} %param.7, bf16[1,48,8192]{2,0,1:T(2,128)(2,1)S(1)} %all-gather), kind=kOutput, calls=%fused_computation.14 | convolution fusion | flops 880889856 | bytes 19210240 | tf_op jit(solution)/shard_map/dot_general | solution.py:25
  32.6 0.0 copy-start.1
  32.6 14.5 %fusion = bf16[8,768]{1,0:T(8,128)(2,1)S(1)} fusion(bf16[48,768]{1,0:T(8,128)(2,1)S(1)} %fusion.21), kind=kCustom, calls=%all-reduce-scatter | all-reduce-scatter fusion | flops 49153 | bytes 86528
  47.1 1.3 collective-permute-start
  48.4 2.0 %collective-permute-start.1 = (bf16[6,768]{1,0:T(8,128)(2,1)S(1)}, bf16[6,768]{1,0:T(8,128)(2,1)S(1)}, u32[]{:S(2)}, u32[]{:S(2)}) collective-permute-start(bf16[6,768]{1,0:T(8,128)(2,1)S(1)} %slice), channel_id=1, source_target_pairs={{0,2},{1,3},{2,4},{3,5},{4,6},{5,7},{8,10},{9,11},{10,12},{11,13},... | collective-permute-start | bytes 27656
  50.4 0.0 copy-done.3
  50.4 0.6 dynamic-slice.4
  51.7 0.1 collective-permute-done.1
  51.8 0.0 collective-permute-done
  51.8 0.2 concatenate
  52.1 0.0 copy-done.4
  52.1 0.3 fusion.24
  52.4 0.7 copy.25
  53.1 0.0 reduce-scatter.4.cloned.1.call-update
  53.1 0.0 all-reduce.4.cloned.1.call-start
  53.2 23.2 %reduce-scatter.4.cloned.1.call-done = bf16[6,2048]{1,0:T(8,128)(2,1)} async-done(((bf16[6,8192]{1,0:T(8,128)(2,1)}), bf16[6,2048]{1,0:T(8,128)(2,1)}) %reduce-scatter.4.cloned.1.call-update) | async-done | bytes 24592 | tf_op jit(solution)/shard_map/reduce_scatter | solution.py:33
  76.4 0.0 copy-done.2
  76.4 0.8 fusion.35
  77.1 9.3 %all-gather.1 = bf16[8,6,2048]{2,1,0:T(8,128)(2,1)S(1)} all-gather(bf16[1,6,2048]{2,1,0:T(8,128)(2,1)S(1)} %fusion.35), channel_id=1, replica_groups=mesh['dom'=4,'col'=8] {'col'}, dimensions={0}, use_global_device_ids=true | all-gather | bytes 221184 | tf_op jit(solution)/shard_map/all_gather | solution.py:38
  86.4 0.1 reshape.30
  86.5 3.0 %convolution_convert_fusion = bf16[48,1024]{1,0:T(8,128)(2,1)S(1)} fusion(bf16[48,2048]{1,0:T(8,128)(2,1)S(1)} %reshape.30, bf16[2048,1024]{1,0:T(8,128)(2,1)} %param.11), kind=kOutput, calls=%fused_computation.12 | convolution fusion | flops 201375744 | bytes 4489216 | tf_op jit(solution)/shard_map/dot_general | solution.py:37
  89.5 0.7 all_to_all.26
  90.2 0.0 all-reduce.4.cloned.1.call-update
  90.2 0.0 copy-done.1
  90.2 8.0 %all_to_all.32 = bf16[6,8,1024]{2,0,1:T(8,128)(2,1)S(1)} all-to-all(bf16[6,8,1024]{2,0,1:T(8,128)(2,1)S(1)} %bitcast.65), channel_id=1, replica_groups=mesh['dom'=4,'col'=8] {'col'}, dimensions={1} | all-to-all | bytes 196608 | tf_op jit(solution)/shard_map/all_to_all | solution.py:53
  98.3 24.0 %all-reduce.4.cloned.1.call-done = bf16[8,6,1024]{2,1,0:T(8,128)(2,1)} async-done(((bf16[8,6,1024]{2,1,0:T(8,128)(2,1)}), bf16[8,6,1024]{2,1,0:T(8,128)(2,1)}) %all-reduce.4.cloned.1.call-update) | async-done | bytes 98320 | tf_op jit(solution)/shard_map/psum | solution.py:42
  122.3 3.6 %all-to-all-start.1 = ((bf16[8,6,1024]{2,1,0:T(8,128)(2,1)}), bf16[8,6,1024]{2,1,0:T(8,128)(2,1)S(1)}, u32[]{:S(2)}, u32[]{:S(2)}) async-start(bf16[8,6,1024]{2,1,0:T(8,128)(2,1)} %all-reduce.4.cloned.1.call-done), calls=%async_computation.2 | async-start | bytes 262144 | tf_op jit(solution)/shard_map/all_to_all | solution.py:43
  126.0 5.4 %all-to-all-done.1 = bf16[8,6,1024]{2,1,0:T(8,128)(2,1)S(1)} async-done(((bf16[8,6,1024]{2,1,0:T(8,128)(2,1)}), bf16[8,6,1024]{2,1,0:T(8,128)(2,1)S(1)}, u32[]{:S(2)}, u32[]{:S(2)}) %all-to-all-start.1) | async-done | bytes 98336 | tf_op jit(solution)/shard_map/all_to_all | solution.py:43
  131.4 0.1 copy.16
  131.5 0.2 fusion.28
  131.7 8.3 %all-gather.2 = bf16[8,6,768]{2,1,0:T(8,128)(2,1)S(1)} all-gather(bf16[1,6,768]{2,1,0:T(8,128)(2,1)S(1)} %reshape.31), channel_id=1, replica_groups=mesh['dom'=4,'col'=8] {'col'}, dimensions={0}, use_global_device_ids=true | all-gather | bytes 82944 | tf_op jit(solution)/shard_map/all_gather | solution.py:51
  140.1 0.6 fusion.12
  140.6 10.4 %all_gather.15 = bf16[48,8192]{1,0:T(8,128)(2,1)S(1)} all-gather(bf16[48,1024]{1,0:T(8,128)(2,1)S(1)} %fusion.12), channel_id=1, replica_groups=mesh['dom'=4,'col'=8] {'col'}, dimensions={1}, use_global_device_ids=true | all-gather | bytes 884736 | tf_op jit(solution)/shard_map/all_gather | solution.py:56
  151.0 9.5 %fusion.25 = bf16[1,48,1024]{2,1,0:T(8,128)(2,1)} fusion(bf16[48,8192]{1,0:T(8,128)(2,1)S(1)} %all_gather.15, bf16[1,8192,1024]{2,1,0:T(8,128)(2,1)} %param.7), kind=kOutput, calls=%fused_computation.16 | convolution fusion | flops 805355520 | bytes 17661952 | tf_op jit(solution)/shard_map/dot_general | solution.py:55
  160.5 0.7 copy.28
  (8 shorter events, 0.2 us)
Async XLA Ops:
  7.2 15.9 %copy-start = (bf16[1,1024,768]{2,1,0:T(8,128)(2,1)S(1)}, bf16[1,1024,768]{2,1,0:T(8,128)(2,1)}, u32[]{:S(2)}) copy-start(bf16[1,1024,768]{2,1,0:T(8,128)(2,1)} %param.8) | copy-start | bytes 4718596
  7.2 69.2 %reduce-scatter.4.cloned.1.call-start = ((), (), s32[]{:S(2)}) async-start(), calls=%async_computation.3 | async-start | bytes 163840 | tf_op jit(solution)/shard_map/reduce_scatter | solution.py:33
  23.0 27.4 %copy-start.3 = (u32[32]{0:T(128)S(1)}, u32[32]{0:T(128)}, u32[]{:S(2)}) copy-start(u32[32]{0:T(128)} %constant.7) | copy-start | bytes 388
  23.0 29.0 %copy-start.4 = (s32[1,6]{1,0:T(1,128)S(1)}, s32[1,6]{1,0:T(1,128)}, u32[]{:S(2)}) copy-start(s32[1,6]{1,0:T(1,128)} %param.10) | copy-start | bytes 76
  23.0 53.3 %copy-start.2 = (bf16[6,2048]{1,0:T(8,128)(2,1)S(1)}, bf16[6,2048]{1,0:T(8,128)(2,1)}, u32[]{:S(2)}) copy-start(bf16[6,2048]{1,0:T(8,128)(2,1)} %param.9) | copy-start | bytes 73732
  32.6 57.6 %copy-start.1 = (bf16[1,6,8192]{2,1,0:T(8,128)(2,1)S(1)}, bf16[1,6,8192]{2,1,0:T(8,128)(2,1)}, u32[]{:S(2)}) copy-start(bf16[1,6,8192]{2,1,0:T(8,128)(2,1)} %param.6) | copy-start | bytes 294916
  47.1 4.7 %collective-permute-start = (bf16[8,768]{1,0:T(8,128)(2,1)S(1)}, bf16[8,768]{1,0:T(8,128)(2,1)S(1)}, u32[]{:S(2)}, u32[]{:S(2)}) collective-permute-start(bf16[8,768]{1,0:T(8,128)(2,1)S(1)} %fusion), channel_id=1, source_target_pairs={{0,1},{1,2},{2,3},{3,4},{4,5},{5,6},{6,7},{8,9},{9,10},{10,11},{11... | collective-permute-start | bytes 36872
  48.4 3.4 %collective-permute-start.1 = (bf16[6,768]{1,0:T(8,128)(2,1)S(1)}, bf16[6,768]{1,0:T(8,128)(2,1)S(1)}, u32[]{:S(2)}, u32[]{:S(2)}) collective-permute-start(bf16[6,768]{1,0:T(8,128)(2,1)S(1)} %slice), channel_id=1, source_target_pairs={{0,2},{1,3},{2,4},{3,5},{4,6},{5,7},{8,10},{9,11},{10,12},{11,13},... | collective-permute-start | bytes 27656
  53.1 69.1 %all-reduce.4.cloned.1.call-start = ((), (), s32[]{:S(2)}) async-start(), calls=%async_computation.4 | async-start | bytes 262144 | tf_op jit(solution)/shard_map/psum | solution.py:42
  122.3 9.1 %all-to-all-start.1 = ((bf16[8,6,1024]{2,1,0:T(8,128)(2,1)}), bf16[8,6,1024]{2,1,0:T(8,128)(2,1)S(1)}, u32[]{:S(2)}, u32[]{:S(2)}) async-start(bf16[8,6,1024]{2,1,0:T(8,128)(2,1)} %all-reduce.4.cloned.1.call-done), calls=%async_computation.2 | async-start | bytes 262144 | tf_op jit(solution)/shard_map/all_to_all | solution.py:43
Sparse Core Ops, SparseCore 0:
  53.3 23.0 reduce-scatter.3
  90.3 31.8 all-reduce.3
where the time goes:
time: 169 us; the launch traced here: 168 us
  blocking collectives  65 us (38%)
  waiting for transfers between devices  52.8 us (31%)
  matrix products  23.1 us (14%)
  between operations  14.9 us (9%)
  starting transfers between devices  7.03 us (4%)
  local copies, waits for them, and re-layouts  4.39 us (3%)
    psum x1, waiting for transfers between devices, per_device(): column_total = lax.psum(partial_solution.astype(jnp.bfloat16), 'dom')  24 us
    reduce_scatter x1, waiting for transfers between devices, per_device(): lax.psum_scatter(placed.astype(jnp.bfloat16), 'dom', scatter_dimension=1,...  23.2 us
    all_gather x1, blocking collectives, per_device(): lax.all_gather(rhs_local, 'col', axis=0, tiled=True)  14.6 us
    unnamed x1, blocking collectives  14.5 us
    all_gather x1, blocking collectives, per_device(): lax.all_gather(interior_rhs, 'col', axis=1, tiled=True)  10.4 us
    dot_general x1, matrix products, per_device(): jnp.dot(interior_step, couple, preferred_element_type=jnp.float32)  9.54 us
    dot_general x1, matrix products, per_device(): jnp.dot(lax.all_gather(interior_rhs, 'col', axis=1, tiled=True), inverse,...  9.46 us
    all_gather x1, blocking collectives, per_device(): lax.all_gather(reduced, 'col', axis=0, tiled=True)  9.25 us
  transfers between devices with their start and end apart: 5, of which 4 were waited for; matrix products, arithmetic and copies ran while one was open for 0% of the time, Pallas kernels for 0%

commit v1 on v0

--- a/solution.py
+++ b/solution.py
@@ -40,7 +40,12 @@
         preferred_element_type=jnp.float32,
     )
     column_total = lax.psum(partial_solution.astype(jnp.bfloat16), "dom")
-    solution = lax.all_to_all(column_total, "col", split_axis=0, concat_axis=1, tiled=True)
+    solution = jnp.concatenate(
+        lax.all_to_all(
+            jnp.stack(jnp.split(column_total, lax.axis_size("col"), axis=0)), "col", 0, 0
+        ),
+        axis=1,
+    )
     local_solution = jnp.einsum(
         "kb,rbs->rks",
         onehot.astype(jnp.bfloat16),

time: 169 us -> 179 us (1.059)
  local copies, waits for them, and re-layouts: 4.39 us -> 14.5 us
  blocking collectives: 65 us -> 56.9 us
  waiting for transfers between devices: 52.8 us -> 57.2 us
  starting transfers between devices: 7.03 us -> 10.4 us
    unnamed x20 -> x25, local copies, waits for them, and re-layouts: 3.53 us -> 13 us
    all_to_all x1 -> x0, blocking collectives: 8.04 us -> none  [per_device(): lax.all_to_all(rhs_local, 'col', split_axis=1, concat_axis=0, tiled=True)]
    psum x1, waiting for transfers between devices: 24 us -> 28.5 us  [per_device(): column_total = lax.psum(partial_solution.astype(jnp.bfloat16), 'dom')]
    all_to_all x1 -> x2, starting transfers between devices: 3.64 us -> 7.04 us  [the longest x1 3.66 us: per_device(): lax.all_to_all(jnp.stack(jnp.split(column_total, lax.axis_size('col'), ax...]
    all_to_all x1 -> x2, waiting for transfers between devices: 5.44 us -> 5.44 us  [the longest x1 5.44 us: per_device(): lax.all_to_all(jnp.stack(jnp.split(column_total, lax.axis_size('col'), ax...]
  transfers between devices with their start and end apart: 5 -> 6, of which waited for: 4 -> 4; matrix products, arithmetic and copies ran while one was open for 0% -> 6% of each run, Pallas kernels for 0% -> 0%
where the time goes in v1:
time: 179 us; the launch traced here: 178 us
  waiting for transfers between devices  57.2 us (32%)
  blocking collectives  56.9 us (32%)
  matrix products  23.7 us (13%)
  between operations  14.8 us (8%)
  local copies, waits for them, and re-layouts  14.5 us (8%)
  starting transfers between devices  10.4 us (6%)
    psum x1, waiting for transfers between devices, per_device(): column_total = lax.psum(partial_solution.astype(jnp.bfloat16), 'dom')  28.5 us
    reduce_scatter x1, waiting for transfers between devices, per_device(): lax.psum_scatter(placed.astype(jnp.bfloat16), 'dom', scatter_dimension=1,...  23.2 us
    all_gather x1, blocking collectives, per_device(): lax.all_gather(rhs_local, 'col', axis=0, tiled=True)  14.6 us
    unnamed x1, blocking collectives  14.3 us
    unnamed x25, local copies, waits for them, and re-layouts  13 us
    all_gather x1, blocking collectives, per_device(): lax.all_gather(interior_rhs, 'col', axis=1, tiled=True)  10.4 us
    dot_general x1, matrix products, per_device(): jnp.dot(interior_step, couple, preferred_element_type=jnp.float32)  9.54 us
    dot_general x1, matrix products, per_device(): jnp.dot(lax.all_gather(interior_rhs, 'col', axis=1, tiled=True), inverse,...  9.46 us
  transfers between devices with their start and end apart: 6, of which 4 were waited for; matrix products, arithmetic and copies ran while one was open for 6% of the time, Pallas kernels for 0%

profile of v1, /device:TPU:0, one launch (start us, length us, event | category | flops | bytes accessed | tf_op | source)
XLA Modules:
  0.0 178.4 jit_solution(11070030512985838979)
XLA Ops:
  7.2 0.0 copy-start
  7.2 0.0 reduce-scatter.4.cloned.1.call-start
  7.2 1.2 copy.14
  8.4 14.6 %all-gather = bf16[1,48,8192]{2,0,1:T(2,128)(2,1)S(1)} all-gather(bf16[1,6,8192]{2,0,1:T(2,128)(2,1)S(1)} %copy.14), channel_id=2, replica_groups=mesh['dom'=4,'col'=8] {'col'}, dimensions={1}, use_global_device_ids=true | all-gather | bytes 884736 | tf_op jit(solution)/shard_map/all_gather | solution.py:20
  23.0 0.0 copy-done
  23.0 0.0 copy-start.2
  23.0 0.0 copy-start.3
  23.0 9.5 %fusion.21 = bf16[48,768]{1,0:T(8,128)(2,1)S(1)} fusion(bf16[1,1024,768]{2,1,0:T(8,128)(2,1)S(1)} %copy-done, bf16[1,8192,1024]{2,1,0:T(8,128)(2,1)} %param.7, bf16[1,48,8192]{2,0,1:T(2,128)(2,1)S(1)} %all-gather), kind=kOutput, calls=%fused_computation.14 | convolution fusion | flops 880889856 | bytes 19210240 | tf_op jit(solution)/shard_map/dot_general | solution.py:25
  32.6 14.3 %fusion = bf16[8,768]{1,0:T(8,128)(2,1)S(1)} fusion(bf16[48,768]{1,0:T(8,128)(2,1)S(1)} %fusion.21), kind=kCustom, calls=%all-reduce-scatter | all-reduce-scatter fusion | flops 49153 | bytes 86528
  46.9 1.3 collective-permute-start
  48.2 2.0 %collective-permute-start.1 = (bf16[6,768]{1,0:T(8,128)(2,1)S(1)}, bf16[6,768]{1,0:T(8,128)(2,1)S(1)}, u32[]{:S(2)}, u32[]{:S(2)}) collective-permute-start(bf16[6,768]{1,0:T(8,128)(2,1)S(1)} %slice), channel_id=1, source_target_pairs={{0,2},{1,3},{2,4},{3,5},{4,6},{5,7},{8,10},{9,11},{10,12},{11,13},... | collective-permute-start | bytes 27656
  50.3 0.0 copy-done.2
  50.3 0.6 dynamic-slice.4
  51.5 0.1 collective-permute-done.1
  51.7 0.0 collective-permute-done
  51.7 0.2 concatenate
  51.9 0.0 copy-done.3
  51.9 0.3 fusion.24
  52.2 0.7 copy.24
  53.0 0.0 reduce-scatter.4.cloned.1.call-update
  53.0 0.0 all-reduce.4.cloned.1.call-start
  53.0 23.2 %reduce-scatter.4.cloned.1.call-done = bf16[6,2048]{1,0:T(8,128)(2,1)} async-done(((bf16[6,8192]{1,0:T(8,128)(2,1)}), bf16[6,2048]{1,0:T(8,128)(2,1)}) %reduce-scatter.4.cloned.1.call-update) | async-done | bytes 24592 | tf_op jit(solution)/shard_map/reduce_scatter | solution.py:33
  76.2 0.0 copy-done.1
  76.2 0.8 fusion.35
  77.0 9.3 %all-gather.1 = bf16[8,6,2048]{2,1,0:T(8,128)(2,1)S(1)} all-gather(bf16[1,6,2048]{2,1,0:T(8,128)(2,1)S(1)} %fusion.35), channel_id=1, replica_groups=mesh['dom'=4,'col'=8] {'col'}, dimensions={0}, use_global_device_ids=true | all-gather | bytes 221184 | tf_op jit(solution)/shard_map/all_gather | solution.py:38
  86.2 0.1 reshape.30
  86.3 3.7 %convolution_convert_fusion = bf16[48,1024]{1,0:T(8,128)(2,1)} fusion(bf16[48,2048]{1,0:T(8,128)(2,1)S(1)} %reshape.30, bf16[2048,1024]{1,0:T(8,128)(2,1)} %param.11), kind=kOutput, calls=%fused_computation.12 | convolution fusion | flops 201375744 | bytes 4489216 | tf_op jit(solution)/shard_map/dot_general | solution.py:37
  90.0 0.0 all-reduce.4.cloned.1.call-update
  90.0 3.4 %all-to-all-start = ((bf16[6,8,1024]{2,0,1:T(8,128)(2,1)}), bf16[6,8,1024]{2,0,1:T(8,128)(2,1)S(1)}, u32[]{:S(2)}, u32[]{:S(2)}) async-start(bf16[6,8,1024]{2,0,1:T(8,128)(2,1)} %bitcast), calls=%async_computation | async-start | bytes 262144 | tf_op jit(solution)/shard_map/all_to_all | solution.py:58
  93.4 28.5 %all-reduce.4.cloned.1.call-done = bf16[48,1024]{1,0:T(8,128)(2,1)} async-done(((bf16[48,1024]{1,0:T(8,128)(2,1)}), bf16[48,1024]{1,0:T(8,128)(2,1)}) %all-reduce.4.cloned.1.call-update) | async-done | bytes 98320 | tf_op jit(solution)/shard_map/psum | solution.py:42
  121.9 1.3 constant_dynamic-update-slice_fusion.7
  123.2 1.4 constant_dynamic-update-slice_fusion.6
  124.6 1.4 constant_dynamic-update-slice_fusion.5
  125.9 1.3 constant_dynamic-update-slice_fusion.4
  127.3 1.3 constant_dynamic-update-slice_fusion.3
  128.6 1.4 constant_dynamic-update-slice_fusion.2
  129.9 1.4 constant_dynamic-update-slice_fusion.1
  131.3 1.3 constant_dynamic-update-slice_fusion
  132.6 0.0 all-to-all-done
  132.7 3.7 %all-to-all-start.1 = ((bf16[8,6,1024]{2,1,0:T(8,128)(2,1)}), bf16[8,6,1024]{2,1,0:T(8,128)(2,1)S(1)}, u32[]{:S(2)}, u32[]{:S(2)}) async-start(bf16[8,6,1024]{2,1,0:T(8,128)(2,1)} %constant_dynamic-update-slice_fusion), calls=%async_computation.2 | async-start | bytes 262144 | tf_op jit(solution)/shard_map/all_to_all | solution.py:44
  136.4 5.4 %all-to-all-done.1 = bf16[8,6,1024]{2,1,0:T(8,128)(2,1)S(1)} async-done(((bf16[8,6,1024]{2,1,0:T(8,128)(2,1)}), bf16[8,6,1024]{2,1,0:T(8,128)(2,1)S(1)}, u32[]{:S(2)}, u32[]{:S(2)}) %all-to-all-start.1) | async-done | bytes 98336 | tf_op jit(solution)/shard_map/all_to_all | solution.py:44
  141.8 0.1 copy.15
  141.9 0.2 fusion.28
  142.2 8.3 %all-gather.2 = bf16[8,6,768]{2,1,0:T(8,128)(2,1)S(1)} all-gather(bf16[1,6,768]{2,1,0:T(8,128)(2,1)S(1)} %reshape.31), channel_id=1, replica_groups=mesh['dom'=4,'col'=8] {'col'}, dimensions={0}, use_global_device_ids=true | all-gather | bytes 82944 | tf_op jit(solution)/shard_map/all_gather | solution.py:56
  150.5 0.6 fusion.12
  151.1 10.4 %all_gather.15 = bf16[48,8192]{1,0:T(8,128)(2,1)S(1)} all-gather(bf16[48,1024]{1,0:T(8,128)(2,1)S(1)} %fusion.12), channel_id=1, replica_groups=mesh['dom'=4,'col'=8] {'col'}, dimensions={1}, use_global_device_ids=true | all-gather | bytes 884736 | tf_op jit(solution)/shard_map/all_gather | solution.py:61
  161.4 9.5 %fusion.25 = bf16[1,48,1024]{2,1,0:T(8,128)(2,1)} fusion(bf16[48,8192]{1,0:T(8,128)(2,1)S(1)} %all_gather.15, bf16[1,8192,1024]{2,1,0:T(8,128)(2,1)} %param.7), kind=kOutput, calls=%fused_computation.16 | convolution fusion | flops 805355520 | bytes 17661952 | tf_op jit(solution)/shard_map/dot_general | solution.py:60
  170.9 0.7 copy.34
  (9 shorter events, 0.2 us)
Async XLA Ops:
  7.2 15.9 %copy-start = (bf16[1,1024,768]{2,1,0:T(8,128)(2,1)S(1)}, bf16[1,1024,768]{2,1,0:T(8,128)(2,1)}, u32[]{:S(2)}) copy-start(bf16[1,1024,768]{2,1,0:T(8,128)(2,1)} %param.8) | copy-start | bytes 4718596
  7.2 69.0 %reduce-scatter.4.cloned.1.call-start = ((), (), s32[]{:S(2)}) async-start(), calls=%async_computation.3 | async-start | bytes 163840 | tf_op jit(solution)/shard_map/reduce_scatter | solution.py:33
  23.0 27.2 %copy-start.2 = (u32[32]{0:T(128)S(1)}, u32[32]{0:T(128)}, u32[]{:S(2)}) copy-start(u32[32]{0:T(128)} %constant.7) | copy-start | bytes 388
  23.0 28.9 %copy-start.3 = (s32[1,6]{1,0:T(1,128)S(1)}, s32[1,6]{1,0:T(1,128)}, u32[]{:S(2)}) copy-start(s32[1,6]{1,0:T(1,128)} %param.10) | copy-start | bytes 76
  23.0 53.2 %copy-start.1 = (bf16[6,2048]{1,0:T(8,128)(2,1)S(1)}, bf16[6,2048]{1,0:T(8,128)(2,1)}, u32[]{:S(2)}) copy-start(bf16[6,2048]{1,0:T(8,128)(2,1)} %param.9) | copy-start | bytes 73732
  46.9 4.7 %collective-permute-start = (bf16[8,768]{1,0:T(8,128)(2,1)S(1)}, bf16[8,768]{1,0:T(8,128)(2,1)S(1)}, u32[]{:S(2)}, u32[]{:S(2)}) collective-permute-start(bf16[8,768]{1,0:T(8,128)(2,1)S(1)} %fusion), channel_id=1, source_target_pairs={{0,1},{1,2},{2,3},{3,4},{4,5},{5,6},{6,7},{8,9},{9,10},{10,11},{11... | collective-permute-start | bytes 36872
  48.2 3.4 %collective-permute-start.1 = (bf16[6,768]{1,0:T(8,128)(2,1)S(1)}, bf16[6,768]{1,0:T(8,128)(2,1)S(1)}, u32[]{:S(2)}, u32[]{:S(2)}) collective-permute-start(bf16[6,768]{1,0:T(8,128)(2,1)S(1)} %slice), channel_id=1, source_target_pairs={{0,2},{1,3},{2,4},{3,5},{4,6},{5,7},{8,10},{9,11},{10,12},{11,13},... | collective-permute-start | bytes 27656
  53.0 68.9 %all-reduce.4.cloned.1.call-start = ((), (), s32[]{:S(2)}) async-start(), calls=%async_computation.4 | async-start | bytes 196608 | tf_op jit(solution)/shard_map/psum | solution.py:42
  90.0 42.6 %all-to-all-start = ((bf16[6,8,1024]{2,0,1:T(8,128)(2,1)}), bf16[6,8,1024]{2,0,1:T(8,128)(2,1)S(1)}, u32[]{:S(2)}, u32[]{:S(2)}) async-start(bf16[6,8,1024]{2,0,1:T(8,128)(2,1)} %bitcast), calls=%async_computation | async-start | bytes 262144 | tf_op jit(solution)/shard_map/all_to_all | solution.py:58
  132.7 9.2 %all-to-all-start.1 = ((bf16[8,6,1024]{2,1,0:T(8,128)(2,1)}), bf16[8,6,1024]{2,1,0:T(8,128)(2,1)S(1)}, u32[]{:S(2)}, u32[]{:S(2)}) async-start(bf16[8,6,1024]{2,1,0:T(8,128)(2,1)} %constant_dynamic-update-slice_fusion), calls=%async_computation.2 | async-start | bytes 262144 | tf_op jit(solution)/shard_map/all_to_all | solution.py:44
Sparse Core Ops, SparseCore 0:
  53.1 23.0 reduce-scatter.3
  90.1 31.6 all-reduce.3
